TPU v7x, 32 devices: a whole 2x2x4 slice. The times are simulated.
32 devices in a mesh: south: 8 (over z, x), east: 4 (over y, core).
Axes of the slice: x: 2, y: 2, z: 4, core: 2. Of those that a mesh axis runs over, the one named last changes fastest.
Arguments:
- tracer: float32 [256, 128, 128], P('south', 'east'), may hold values from 0.2 to 1.8
- flow_j: float32 [256, 128, 128], P('south', 'east'), may hold values from -0.3 to 0.3
- flow_i: float32 [256, 128, 128], P('south', 'east'), may hold values from -0.3 to 0.3
Outputs:
- running_total: float32 [256, 128, 128], P('south', 'east')
- tracer_end: float32 [256, 128, 128], P('south', 'east')
All inputs are finite; a program needn't handle non-finite values.
Results may differ from a plain program's by a relative error of at most 0.00002.
Values sent between devices are 32-bit elements; how exact they have to be, the bound alone decides.
A program may use at most 64 MiB of HBM per device.

v0:
```python
import functools

import jax
import jax.numpy as jnp
from jax import lax
from jax.experimental import pallas as pl
from jax.experimental.pallas import tpu as pltpu
from jax.sharding import PartitionSpec as P

RATE = 0.05
PAD = 2
TILE = 8
MESH = pl.DeviceIdType.MESH
LOWER, UPPER, LEFT, RIGHT = range(4)
SIDES = ((-1, 0), (1, 0), (0, -1), (0, 1))
BACK = (UPPER, LOWER, RIGHT, LEFT)


def chunk_of(rows, most):
    return max(c for c in range(1, most + 1) if rows % c == 0)


def view(ref, row, rows, col, cols):
    return ref.at[pl.ds(row + PAD, rows), pl.ds(col + TILE, cols), :]


def line(ref, row, col, cols):
    return ref[row + PAD, pl.ds(col + TILE, cols), :]


def step(middle, lower_j, upper_j, lower_i, upper_i, flow_j, flow_i):
    spread = lower_j + upper_j + lower_i + upper_i - 4.0 * middle
    return middle - flow_j * (upper_j - lower_j) - flow_i * (upper_i - lower_i) + RATE * spread


def advance(level, flows, row, rows, col, cols):
    def at(dj, di):
        return view(level, row + dj, rows, col + di, cols)[...]

    return step(at(0, 0), at(-1, 0), at(1, 0), at(0, -1), at(0, 1),
                view(flows.at[0], row, rows, col, cols)[...], view(flows.at[1], row, rows, col, cols)[...])


def kernel(souths, easts, tracer, flow_j, flow_i, before, end, level0, level1, level2, level3, flows, halo, reply, spill,
           own, totals, ready, load_sem, send_sem, late_sem, tracer_sem, flow_sem, far_sem, step_sem, total_send, total_recv):
    J, I, M = tracer.shape
    s, e = lax.axis_index("south"), lax.axis_index("east")
    levels = (level0, level1, level2, level3)
    zeros = functools.partial(jnp.zeros, dtype=jnp.float32)
    loads = [pltpu.make_async_copy(src, view(dst, 0, J, 0, I), load_sem.at[k])
             for k, (src, dst) in enumerate(((tracer, level0), (flow_j, flows.at[0]), (flow_i, flows.at[1])))]
    for load in loads:
        load.start()
    exists = (s > 0, s < souths - 1, e > 0, e < easts - 1)

    def peer(side):
        return {"south": s + SIDES[side][0], "east": e + SIDES[side][1]}

    barrier = pltpu.get_barrier_semaphore()
    near = 0
    for side in range(4):
        near = near + exists[side].astype(jnp.int32)

        @pl.when(exists[side])
        def _(side=side):
            pl.semaphore_signal(barrier, inc=1, device_id=peer(side), device_id_type=MESH)

    stages, known = [], 1
    while known < souths - 1:
        stages.append(known)
        known *= 2

    def tell(stage):
        reach = stages[stage]
        for ok, other in ((s >= reach, s - reach), (s + reach < souths, s + reach)):
            @pl.when(ok)
            def _(other=other):
                pl.semaphore_signal(ready.at[stage], inc=1, device_id={"south": other, "east": e}, device_id_type=MESH)

    def hear(stage):
        reach = stages[stage]
        pl.semaphore_wait(ready.at[stage], (s >= reach).astype(jnp.int32) + (s + reach < souths).astype(jnp.int32))

    def clear(level, row, rows, col, cols):
        view(level, row, rows, col, cols)[...] = zeros((rows, cols, M))

    def trim(k, row, rows, wide):
        for side, col in ((LEFT, -wide), (RIGHT, I)):
            pl.when(jnp.logical_not(exists[side]))(lambda col=col: clear(levels[k], row, rows, col, wide))

    with jax.named_scope("clear"):
        clear(level2, -2, 2, -2, I + 4)
        clear(level2, J, 2, -2, I + 4)
        clear(level3, -2, 1, 0, I)
        clear(level3, J + 1, 1, 0, I)
        spill[...] = zeros(spill.shape)
        for side, row in ((LOWER, -2), (UPPER, J)):
            pl.when(jnp.logical_not(exists[side]))(lambda row=row: clear(level0, row, 2, -3, I + 6))
        trim(0, 0, J, 4)
    with jax.named_scope("barw"):
        pl.semaphore_wait(barrier, near)

    def remote(side, src, dst, send, recv):
        return pltpu.make_async_remote_copy(src_ref=src, dst_ref=dst, send_sem=send, recv_sem=recv,
                                            device_id=peer(side), device_id_type=MESH)

    def block(ref, side, at_home, row, rows, col, cols):
        if side in (LOWER, UPPER):
            row = {(LOWER, True): row, (LOWER, False): J + row,
                   (UPPER, True): J - row - rows, (UPPER, False): -row - rows}[side, at_home]
        else:
            col = {(LEFT, True): col, (LEFT, False): I + col,
                   (RIGHT, True): I - col - cols, (RIGHT, False): -col - cols}[side, at_home]
        if len(ref.shape) == 4:
            return ref.at[:, pl.ds(row + PAD, rows), pl.ds(col + TILE, cols), :]
        return view(ref, row, rows, col, cols)

    def shift(side, ref, sems, *area):
        return remote(side, block(ref, side, True, *area), block(ref, side, False, *area), send_sem.at[side], sems.at[side])

    def first_tracer(side):
        if side in (LOWER, UPPER):
            return shift(side, level0, far_sem, 0, 2, 0, I)
        return shift(side, level0, tracer_sem, 0, J, 0, 4)

    def first_flows(side):
        if side in (LOWER, UPPER):
            return [shift(side, flows, far_sem, 0, 1, 0, I), shift(side, flows.at[0], far_sem, 1, 1, 0, I)]
        return [shift(side, flows, flow_sem, 0, J, 0, 3)]

    def corners(side, name):
        if name == "tracer":
            return [shift(side, level0, far_sem, 0, 2, col, 3) for col in (-3, I)]
        return [shift(side, flows, far_sem, 0, 1, col, 2) for col in (-2, I)]

    def second(side):
        row = {LOWER: 0, UPPER: J - 2}[side]
        return remote(side, view(level2, row, 2, -1, I + 2), halo.at[BACK[side], :, pl.ds(TILE - 1, I + 2), :],
                      late_sem.at[side], step_sem.at[side])

    def start(side, make):
        @pl.when(exists[side])
        def _():
            copies = make()
            for copy in copies if isinstance(copies, list) else [copies]:
                copy.start()

    def drain(sem, rows, cols):
        part = level0.at[pl.ds(0, rows), pl.ds(0, cols), :]
        pltpu.make_async_copy(part, part, sem).wait()

    def update(k, row, rows, col, cols):
        value = advance(levels[k - 1], flows, row, rows, col, cols)
        if k == 4:
            end[pl.ds(row, rows), pl.ds(col, cols), :] = value
        else:
            view(levels[k], row, rows, col, cols)[...] = value

    def sweep(k, first, last, col, cols, most):
        rows = chunk_of(last - first, most)

        def body(turn, _):
            update(k, first + turn * rows, rows, col, cols)
            return 0

        lax.fori_loop(0, (last - first) // rows, body, 0)

    with jax.named_scope("loads"):
        loads[0].wait()
        for side in (LOWER, UPPER, LEFT, RIGHT):
            start(side, lambda side=side: first_tracer(side))
        loads[1].wait()
        loads[2].wait()
    with jax.named_scope("startf"):
        for side in (LOWER, UPPER, LEFT, RIGHT):
            start(side, lambda side=side: first_flows(side))
        if stages:
            tell(0)
    with jax.named_scope("recvi"):
        for side in (LEFT, RIGHT):
            pl.when(exists[side])(lambda side=side: shift(BACK[side], level0, tracer_sem, 0, J, 0, 4).wait_recv())
        for side in (LOWER, UPPER):
            start(side, lambda side=side: corners(side, "tracer"))
    with jax.named_scope("recvif"):
        for side in (LEFT, RIGHT):
            pl.when(exists[side])(lambda side=side: shift(BACK[side], flows, flow_sem, 0, J, 0, 3).wait_recv())
        for side in (LOWER, UPPER):
            start(side, lambda side=side: corners(side, "flows"))
    for stage in range(1, len(stages)):
        hear(stage - 1)
        tell(stage)

    with jax.named_scope("middle"):
        for k in range(1, 5):
            sweep(k, k, J - k, k - 4, I + 2 * (4 - k), 7)
            if k < 4:
                trim(k, k, J - 2 * k, 4 - k)
        total = end[4]
        for row in range(5, J - 4):
            total = total + end[row]

    with jax.named_scope("recvj"):
        for side in (LOWER, UPPER):
            pl.when(exists[side])(lambda side=side: drain(far_sem.at[BACK[side]], 5, I + 4))
    with jax.named_scope("rim2"):
        for inner, outer in ((0, -1), (J - 1, J)):
            update(1, inner, 1, -3, I + 6)
            update(1, outer, 1, -2, I + 4)
            trim(1, inner, 1, 3)
            trim(1, outer, 1, 2)
        for side, outer in ((LOWER, -1), (UPPER, J)):
            pl.when(jnp.logical_not(exists[side]))(lambda outer=outer: clear(level1, outer, 1, -2, I + 4))
        for side, row in ((LOWER, 0), (UPPER, J - 2)):
            update(2, row, 2, -2, I + 4)
            trim(2, row, 2, 2)
            start(side, lambda side=side: second(side))
    with jax.named_scope("rim4"):
        for side, row, outer in ((LOWER, -1, -1), (UPPER, J - 3, J)):
            update(3, row, 4, -1, I + 2)
            trim(3, row, 4, 1)
            pl.when(jnp.logical_not(exists[side]))(lambda outer=outer: clear(level3, outer, 1, -1, I + 2))
        for side, row, outer, last, sign in ((LOWER, 0, -1, -2, -1.0), (UPPER, J - 4, J, J + 1, 1.0)):
            update(4, row, 4, 0, I)
            for r in range(4):
                total = total + end[row + r]

            @pl.when(exists[side])
            def _(side=side, outer=outer, last=last, sign=sign):
                value = advance(level3, flows, outer, 1, 0, I)[0]
                spill[side] = value + (RATE + sign * line(flows.at[0], last, 0, I)) * line(level3, outer, 0, I)

        own[...] = total + spill[LOWER] + spill[UPPER]

    def total_copy(source, other):
        return pltpu.make_async_remote_copy(
            src_ref=own, dst_ref=totals.at[source], send_sem=total_send, recv_sem=total_recv,
            device_id={"south": other, "east": e}, device_id_type=MESH)

    with jax.named_scope("give"):
        if stages:
            hear(len(stages) - 1)

        def give(turn, _):
            total_copy(s, s + turn).start()
            return 0

        lax.fori_loop(1, souths - s, give, 0)

    with jax.named_scope("recv2"):
        for side in (LOWER, UPPER):
            pl.when(exists[side])(lambda side=side: second(BACK[side]).wait_recv())
    with jax.named_scope("reply"):
        for side, sign, edge, inner, outer, close, away in (
            (LOWER, 1.0, 0, 1, -1, 1, 0), (UPPER, -1.0, J - 1, J - 2, J, 0, 1),
        ):
            @pl.when(exists[side])
            def _(side=side, sign=sign, edge=edge, inner=inner, outer=outer, close=close, away=away):
                def near_at(di, cols=I, col=0):
                    return halo[side, close, pl.ds(TILE + col + di, cols), :]

                def pair(value, at_outer):
                    none = jnp.zeros_like(value)
                    lower = (side == LOWER)
                    return (value, none) if lower else (none, value)

                reply[side, pl.ds(TILE - 1, I + 2), :] = (
                    RATE + sign * line(flows.at[0], edge, -1, I + 2)) * near_at(0, I + 2, -1)
                far = halo[side, away, pl.ds(TILE, I), :]
                outside = step(near_at(0), *pair(far, True), near_at(-1), near_at(1),
                               line(flows.at[0], outer, 0, I), line(flows.at[1], outer, 0, I))

                def here(di):
                    return reply[side, pl.ds(TILE + di, I), :]

                first = step(here(0), *pair(outside, False), here(-1), here(1),
                             line(flows.at[0], edge, 0, I), line(flows.at[1], edge, 0, I))
                then = (RATE + sign * line(flows.at[0], inner, 0, I)) * here(0)
                end[edge] = end[edge] + first
                end[inner] = end[inner] + then
                if side == LOWER:
                    spill[LOWER] = spill[LOWER] - first - then

    with jax.named_scope("sent"):
        for side in range(4):
            rows, cols = (5, I + 4) if side in (LOWER, UPPER) else (J, 10)
            pl.when(exists[side])(lambda side=side, rows=rows, cols=cols: drain(send_sem.at[side], rows, cols))
        for side in (LOWER, UPPER):
            pl.when(exists[side])(lambda side=side: second(side).wait_send())
    with jax.named_scope("take"):
        for count in range(1, souths):
            part = totals.at[pl.ds(0, count)]
            pl.when(s == count)(lambda part=part: pltpu.make_async_copy(part, part, total_recv).wait())
        before[...] = lax.fori_loop(0, s, lambda source, state: state + totals[source], spill[LOWER])
    for count in range(1, souths):
        part = totals.at[pl.ds(0, count)]
        pl.when(s == souths - 1 - count)(lambda part=part: pltpu.make_async_copy(part, part, total_send).wait())


def write_out(scale, before, end, running_out, end_out, running, sems):
    J = end.shape[0]
    parts = 2 if J % 2 == 0 else 1
    rows = J // parts
    copies = [pltpu.make_async_copy(end, end_out, sems.at[0])]
    copies[0].start()
    state = before[...]
    for part in range(parts):
        for row in range(part * rows, (part + 1) * rows):
            state = state + end[row]
            running[row] = state * scale
        area = pl.ds(part * rows, rows)
        copies.append(pltpu.make_async_copy(running.at[area], running_out.at[area], sems.at[1 + part]))
        copies[-1].start()
    for copy in copies:
        copy.wait()


def per_device(souths, easts, tracer, flow_j, flow_i):
    J, I, M = tracer.shape
    out = jax.ShapeDtypeStruct((J, I, M), jnp.float32)
    padded = (J + 2 * PAD, I + 2 * TILE, M)
    dma = pltpu.SemaphoreType.DMA
    results = pl.pallas_call(
        functools.partial(kernel, souths, easts),
        out_shape=(jax.ShapeDtypeStruct((I, M), jnp.float32), out),
        in_specs=[pl.BlockSpec(memory_space=pl.ANY)] * 3,
        out_specs=(pl.BlockSpec(memory_space=pltpu.VMEM),) * 2,
        scratch_shapes=[pltpu.VMEM(padded, jnp.float32)] * 4
        + [
            pltpu.VMEM((2,) + padded, jnp.float32),
            pltpu.VMEM((2, 2) + padded[1:], jnp.float32),
            pltpu.VMEM((2,) + padded[1:], jnp.float32),
            pltpu.VMEM((2, I, M), jnp.float32),
            pltpu.VMEM((I, M), jnp.float32),
            pltpu.VMEM((souths, I, M), jnp.float32),
            pltpu.SemaphoreType.REGULAR((max(1, (souths - 1).bit_length()),)),
            dma((3,)), dma((4,)), dma((2,)), dma((4,)), dma((4,)), dma((2,)), dma((2,)), dma, dma,
        ],
        compiler_params=pltpu.CompilerParams(collective_id=0, has_side_effects=True,
                                             vmem_limit_bytes=106 * 2 ** 19),
    )(tracer, flow_j, flow_i)
    return pl.pallas_call(
        functools.partial(write_out, 1.0 / (J * souths)),
        out_shape=(out, out),
        in_specs=[pl.BlockSpec(memory_space=pltpu.VMEM)] * 2,
        out_specs=(pl.BlockSpec(memory_space=pl.ANY),) * 2,
        scratch_shapes=[pltpu.VMEM((J, I, M), jnp.float32), pltpu.SemaphoreType.DMA((3,))],
        compiler_params=pltpu.CompilerParams(vmem_limit_bytes=2 ** 21),
    )(*results)


def solution(mesh):
    spec = P("south", "east", None)
    body = functools.partial(per_device, mesh.shape["south"], mesh.shape["east"])
    return jax.shard_map(body, mesh=mesh, in_specs=(spec,) * 3, out_specs=(spec,) * 2, check_vma=False)
```

profile of v0, /device:TPU:25, one launch (start us, length us, event | category | flops | bytes accessed | tf_op | source)
XLA Modules:
  0.0 15.0 jit_solution(11248568638931147461)
XLA Ops:
  0.6 13.4 %shard_map.50 = (f32[32,128]{1,0:T(8,128)S(1)}, f32[32,32,128]{2,1,0:T(8,128)S(1)}) custom-call(f32[32,32,128]{2,1,0:T(8,128)} %tracer.1, f32[32,32,128]{2,1,0:T(8,128)} %flow_j.1, f32[32,32,128]{2,1,0:T(8,128)} %flow_i.1), custom_call_target="tpu_custom_call" | custom-call | tf_op jit(solution)/shard_map/pallas_call | solution.py:322
  14.0 1.0 %shard_map.51 = (f32[32,32,128]{2,1,0:T(8,128)}, f32[32,32,128]{2,1,0:T(8,128)}) custom-call(f32[32,128]{1,0:T(8,128)S(1)} %get-tuple-element.4.before, f32[32,32,128]{2,1,0:T(8,128)S(1)} %get-tuple-element.5.end), custom_call_target="tpu_custom_call" | custom-call | tf_op jit(solution)/shard_map/pallas_call | solution.py:341
where the time goes:
time: 15.2 us; the launch traced here: 15 us
  Pallas kernels  14.4 us (95%)
  between operations  0.64 us (4%)
    pallas_call x1, Pallas kernels, per_device(): pl.pallas_call(functools.partial(kernel, souths, easts), out_shape=(jax.S...  13.4 us
    pallas_call x1, Pallas kernels, per_device(): pl.pallas_call(functools.partial(write_out, 1.0 / (J * souths)), out_shap...  0.99 us

commit v1 on v0

--- a/solution.py
+++ b/solution.py
@@ -42,15 +42,18 @@
 
 
 def kernel(souths, easts, tracer, flow_j, flow_i, before, end, level0, level1, level2, level3, flows, halo, reply, spill,
-           own, totals, ready, load_sem, send_sem, late_sem, tracer_sem, flow_sem, far_sem, step_sem, total_send, total_recv):
+           tracer_bits, flow_bits, own, totals, ready, load_sem, send_sem, late_sem, bits_sem, side_sem, far_sem, last_sem,
+           step_sem, total_send, total_recv):
     J, I, M = tracer.shape
     s, e = lax.axis_index("south"), lax.axis_index("east")
     levels = (level0, level1, level2, level3)
     zeros = functools.partial(jnp.zeros, dtype=jnp.float32)
-    loads = [pltpu.make_async_copy(src, view(dst, 0, J, 0, I), load_sem.at[k])
-             for k, (src, dst) in enumerate(((tracer, level0), (flow_j, flows.at[0]), (flow_i, flows.at[1])))]
-    for load in loads:
-        load.start()
+    fields = ((tracer, level0), (flow_j, flows.at[0]), (flow_i, flows.at[1]))
+    for number, part, bands in ((0, fields[:1], ((0, 2), (J - 2, 2))), (1, fields[1:], ((0, 2), (J - 2, 2))),
+                                (2, fields[:1], ((2, J - 4),)), (3, fields[1:], ((2, J - 4),))):
+        for src, dst in part:
+            for row, rows in bands:
+                pltpu.make_async_copy(src.at[pl.ds(row, rows)], view(dst, row, rows, 0, I), load_sem.at[number]).start()
     exists = (s > 0, s < souths - 1, e > 0, e < easts - 1)
 
     def peer(side):
@@ -84,8 +87,9 @@
     def clear(level, row, rows, col, cols):
         view(level, row, rows, col, cols)[...] = zeros((rows, cols, M))
 
-    def trim(k, row, rows, wide):
-        for side, col in ((LEFT, -wide), (RIGHT, I)):
+    def trim(k, row, rows, wide, sides=(LEFT, RIGHT)):
+        for side in sides:
+            col = {LEFT: -wide, RIGHT: I}[side]
             pl.when(jnp.logical_not(exists[side]))(lambda col=col: clear(levels[k], row, rows, col, wide))
 
     with jax.named_scope("clear"):
@@ -118,20 +122,43 @@
     def shift(side, ref, sems, *area):
         return remote(side, block(ref, side, True, *area), block(ref, side, False, *area), send_sem.at[side], sems.at[side])
 
-    def first_tracer(side):
-        if side in (LOWER, UPPER):
-            return shift(side, level0, far_sem, 0, 2, 0, I)
-        return shift(side, level0, tracer_sem, 0, J, 0, 4)
-
-    def first_flows(side):
-        if side in (LOWER, UPPER):
-            return [shift(side, flows, far_sem, 0, 1, 0, I), shift(side, flows.at[0], far_sem, 1, 1, 0, I)]
-        return [shift(side, flows, flow_sem, 0, J, 0, 3)]
-
-    def corners(side, name):
-        if name == "tracer":
-            return [shift(side, level0, far_sem, 0, 2, col, 3) for col in (-3, I)]
-        return [shift(side, flows, far_sem, 0, 1, col, 2) for col in (-2, I)]
+    def far_tracer(side):
+        return [shift(side, level0, far_sem, 0, 2, 0, I)]
+
+    def far_flows(side):
+        return [shift(side, flows, far_sem, 0, 1, 0, I)]
+
+    def far_last(side):
+        return [shift(side, flows.at[0], last_sem, 1, 1, 0, I)]
+
+    def side_tracer(side):
+        return [shift(side, level0, side_sem, 0, J, 0, 4)]
+
+    def side_flows(side):
+        return [shift(side, flows, side_sem, 0, J, 0, 3)]
+
+    bands = (LOWER, UPPER)
+
+    def bits(side):
+        out = []
+        for band in bands:
+            at = {LEFT: 0, RIGHT: I - 3}[side], {LEFT: 0, RIGHT: I - 2}[side]
+            to = BACK[side] - LEFT
+            out += [remote(side, view(level0, (0, J - 2)[band], 2, at[0], 3), tracer_bits.at[to, band, :, pl.ds(0, 3), :],
+                           send_sem.at[side], bits_sem.at[to]),
+                    remote(side, flows.at[:, pl.ds((0, J - 1)[band] + PAD, 1), pl.ds(at[1] + TILE, 2), :],
+                           flow_bits.at[to, band, :, :, pl.ds(0, 2), :], send_sem.at[side], bits_sem.at[to])]
+        return out
+
+    def relay(band, side, here):
+        to = side - LEFT
+        row = (J, -2)[band], (J, -1)[band]
+        col = {LEFT: -3, RIGHT: I}[side], {LEFT: -2, RIGHT: I}[side]
+        src = ((tracer_bits.at[to, band, :, pl.ds(0, 3), :], flow_bits.at[to, band, :, :, pl.ds(0, 2), :]) if here else
+               (view(level0, (0, J - 2)[band], 2, col[0], 3),
+                flows.at[:, pl.ds((0, J - 1)[band] + PAD, 1), pl.ds(col[1] + TILE, 2), :]))
+        dst = (view(level0, row[0], 2, col[0], 3), flows.at[:, pl.ds(row[1] + PAD, 1), pl.ds(col[1] + TILE, 2), :])
+        return [remote(band, a, b, send_sem.at[band], far_sem.at[band]) for a, b in zip(src, dst)]
 
     def second(side):
         row = {LOWER: 0, UPPER: J - 2}[side]
@@ -141,12 +168,11 @@
     def start(side, make):
         @pl.when(exists[side])
         def _():
-            copies = make()
-            for copy in copies if isinstance(copies, list) else [copies]:
+            for copy in make():
                 copy.start()
 
-    def drain(sem, rows, cols):
-        part = level0.at[pl.ds(0, rows), pl.ds(0, cols), :]
+    def drain(sem, rows, cols, ref=None):
+        part = (level0 if ref is None else ref).at[..., pl.ds(0, rows), pl.ds(0, cols), :]
         pltpu.make_async_copy(part, part, sem).wait()
 
     def update(k, row, rows, col, cols):
@@ -165,43 +191,76 @@
 
         lax.fori_loop(0, (last - first) // rows, body, 0)
 
-    with jax.named_scope("loads"):
-        loads[0].wait()
-        for side in (LOWER, UPPER, LEFT, RIGHT):
-            start(side, lambda side=side: first_tracer(side))
-        loads[1].wait()
-        loads[2].wait()
-    with jax.named_scope("startf"):
-        for side in (LOWER, UPPER, LEFT, RIGHT):
-            start(side, lambda side=side: first_flows(side))
+    def both(*makes, sides=(LOWER, UPPER)):
+        for turn in range(2):
+            @pl.when(lax.rem(s, 2) == turn)
+            def _(turn=turn):
+                for side in (sides if turn == 0 else sides[::-1]):
+                    start(side, lambda side=side: [copy for make in makes for copy in make(side)])
+
+    def share(side):
+        for here in (True, False):
+            @pl.when(exists[side] if here else jnp.logical_not(exists[side]))
+            def _(here=here):
+                if here:
+                    drain(bits_sem.at[side - LEFT], 5, 4)
+                for band in bands:
+                    start(band, lambda band=band: relay(band, side, here))
+
+    def strip(side):
+        pl.when(exists[side])(lambda: drain(side_sem.at[BACK[side]], J, 10))
+        for k in range(1, 5):
+            sweep(k, k, J - k, {LEFT: k - 4, RIGHT: I - k}[side], 4, 15)
+            if k < 4:
+                trim(k, k, J - 2 * k, 4 - k, (side,))
+
+    with jax.named_scope("load0"):
+        drain(load_sem.at[0], 4, I)
+        both(far_tracer)
+    with jax.named_scope("load1"):
+        drain(load_sem.at[1], 4, I, flows)
+        both(far_flows)
+        for side in (LEFT, RIGHT):
+            start(side, lambda side=side: bits(side))
         if stages:
             tell(0)
-    with jax.named_scope("recvi"):
+    with jax.named_scope("load2"):
+        drain(load_sem.at[2], J - 4, I)
         for side in (LEFT, RIGHT):
-            pl.when(exists[side])(lambda side=side: shift(BACK[side], level0, tracer_sem, 0, J, 0, 4).wait_recv())
-        for side in (LOWER, UPPER):
-            start(side, lambda side=side: corners(side, "tracer"))
-    with jax.named_scope("recvif"):
+            start(side, lambda side=side: side_tracer(side))
+    with jax.named_scope("load3"):
+        drain(load_sem.at[3], J - 4, I, flows)
         for side in (LEFT, RIGHT):
-            pl.when(exists[side])(lambda side=side: shift(BACK[side], flows, flow_sem, 0, J, 0, 3).wait_recv())
-        for side in (LOWER, UPPER):
-            start(side, lambda side=side: corners(side, "flows"))
-    for stage in range(1, len(stages)):
-        hear(stage - 1)
-        tell(stage)
-
-    with jax.named_scope("middle"):
+            start(side, lambda side=side: side_flows(side))
+    with jax.named_scope("inner"):
         for k in range(1, 5):
-            sweep(k, k, J - k, k - 4, I + 2 * (4 - k), 7)
-            if k < 4:
-                trim(k, k, J - 2 * k, 4 - k)
-        total = end[4]
-        for row in range(5, J - 4):
-            total = total + end[row]
+            sweep(k, k, J - k, k, I - 2 * k, 7)
+    for turn, (early, late) in enumerate(((RIGHT, LEFT), (LEFT, RIGHT))):
+        @pl.when(lax.rem(e, 2) == turn)
+        def _(early=early, late=late):
+            with jax.named_scope("early"):
+                share(early)
+                both(far_last)
+                strip(early)
+            with jax.named_scope("hear0"):
+                for stage in range(1, len(stages) - 1):
+                    hear(stage - 1)
+                    tell(stage)
+            with jax.named_scope("share"):
+                share(late)
+            with jax.named_scope("hear1"):
+                for stage in range(max(1, len(stages) - 1), len(stages)):
+                    hear(stage - 1)
+                    tell(stage)
+            with jax.named_scope("late"):
+                strip(late)
+    total = end[4]
+    for row in range(5, J - 4):
+        total = total + end[row]
 
     with jax.named_scope("recvj"):
         for side in (LOWER, UPPER):
-            pl.when(exists[side])(lambda side=side: drain(far_sem.at[BACK[side]], 5, I + 4))
+            pl.when(exists[side])(lambda side=side: drain(far_sem.at[BACK[side]], 4, I + 5))
     with jax.named_scope("rim2"):
         for inner, outer in ((0, -1), (J - 1, J)):
             update(1, inner, 1, -3, I + 6)
@@ -213,8 +272,10 @@
         for side, row in ((LOWER, 0), (UPPER, J - 2)):
             update(2, row, 2, -2, I + 4)
             trim(2, row, 2, 2)
-            start(side, lambda side=side: second(side))
+            start(side, lambda side=side: [second(side)])
     with jax.named_scope("rim4"):
+        for side in (LOWER, UPPER):
+            pl.when(exists[side])(lambda side=side: drain(last_sem.at[BACK[side]], 1, I))
         for side, row, outer in ((LOWER, -1, -1), (UPPER, J - 3, J)):
             update(3, row, 4, -1, I + 2)
             trim(3, row, 4, 1)
@@ -282,7 +343,7 @@
 
     with jax.named_scope("sent"):
         for side in range(4):
-            rows, cols = (5, I + 4) if side in (LOWER, UPPER) else (J, 10)
+            rows, cols = (5, I + 4) if side in (LOWER, UPPER) else (J + 2, 10)
             pl.when(exists[side])(lambda side=side, rows=rows, cols=cols: drain(send_sem.at[side], rows, cols))
         for side in (LOWER, UPPER):
             pl.when(exists[side])(lambda side=side: second(side).wait_send())
@@ -330,10 +391,12 @@
             pltpu.VMEM((2, 2) + padded[1:], jnp.float32),
             pltpu.VMEM((2,) + padded[1:], jnp.float32),
             pltpu.VMEM((2, I, M), jnp.float32),
+            pltpu.VMEM((2, 2, 2, TILE, M), jnp.float32),
+            pltpu.VMEM((2, 2, 2, 1, TILE, M), jnp.float32),
             pltpu.VMEM((I, M), jnp.float32),
             pltpu.VMEM((souths, I, M), jnp.float32),
             pltpu.SemaphoreType.REGULAR((max(1, (souths - 1).bit_length()),)),
-            dma((3,)), dma((4,)), dma((2,)), dma((4,)), dma((4,)), dma((2,)), dma((2,)), dma, dma,
+            dma((4,)), dma((4,)), dma((2,)), dma((2,)), dma((4,)), dma((2,)), dma((2,)), dma((2,)), dma, dma,
         ],
         compiler_params=pltpu.CompilerParams(collective_id=0, has_side_effects=True,
                                              vmem_limit_bytes=106 * 2 ** 19),

time: 15.2 us -> 14.8 us (0.974)
  the two profiles are of different devices: /device:TPU:25 before, /device:TPU:24 now
where the time goes in v1:
time: 14.8 us; the launch traced here: 14.6 us
  Pallas kernels  14 us (95%)
  between operations  0.64 us (4%)
    pallas_call x1, Pallas kernels, per_device(): pl.pallas_call(functools.partial(kernel, souths, easts), out_shape=(jax.S...  13 us
    pallas_call x1, Pallas kernels, per_device(): pl.pallas_call(functools.partial(write_out, 1.0 / (J * souths)), out_shap...  0.99 us

profile of v1, /device:TPU:24, one launch (start us, length us, event | category | flops | bytes accessed | tf_op | source)
XLA Modules:
  0.0 14.6 jit_solution(14830950987914709314)
XLA Ops:
  0.6 13.0 %shard_map.50 = (f32[32,128]{1,0:T(8,128)S(1)}, f32[32,32,128]{2,1,0:T(8,128)S(1)}) custom-call(f32[32,32,128]{2,1,0:T(8,128)} %tracer.1, f32[32,32,128]{2,1,0:T(8,128)} %flow_j.1, f32[32,32,128]{2,1,0:T(8,128)} %flow_i.1), custom_call_target="tpu_custom_call" | custom-call | tf_op jit(solution)/shard_map/pallas_call | solution.py:383
  13.6 1.0 %shard_map.51 = (f32[32,32,128]{2,1,0:T(8,128)}, f32[32,32,128]{2,1,0:T(8,128)}) custom-call(f32[32,128]{1,0:T(8,128)S(1)} %get-tuple-element.4.before, f32[32,32,128]{2,1,0:T(8,128)S(1)} %get-tuple-element.5.end), custom_call_target="tpu_custom_call" | custom-call | tf_op jit(solution)/shard_map/pallas_call | solution.py:404

commit v2 on v1

--- a/solution.py
+++ b/solution.py
@@ -42,18 +42,12 @@
 
 
 def kernel(souths, easts, tracer, flow_j, flow_i, before, end, level0, level1, level2, level3, flows, halo, reply, spill,
-           tracer_bits, flow_bits, own, totals, ready, load_sem, send_sem, late_sem, bits_sem, side_sem, far_sem, last_sem,
-           step_sem, total_send, total_recv):
+           part, tracer_bits, flow_bits, mine, mine_bits, tally, own, totals, ready, load_sem, bits_sem, side_sem, far_sem, last_sem,
+           step_sem, total_recv):
     J, I, M = tracer.shape
     s, e = lax.axis_index("south"), lax.axis_index("east")
     levels = (level0, level1, level2, level3)
     zeros = functools.partial(jnp.zeros, dtype=jnp.float32)
-    fields = ((tracer, level0), (flow_j, flows.at[0]), (flow_i, flows.at[1]))
-    for number, part, bands in ((0, fields[:1], ((0, 2), (J - 2, 2))), (1, fields[1:], ((0, 2), (J - 2, 2))),
-                                (2, fields[:1], ((2, J - 4),)), (3, fields[1:], ((2, J - 4),))):
-        for src, dst in part:
-            for row, rows in bands:
-                pltpu.make_async_copy(src.at[pl.ds(row, rows)], view(dst, row, rows, 0, I), load_sem.at[number]).start()
     exists = (s > 0, s < souths - 1, e > 0, e < easts - 1)
 
     def peer(side):
@@ -67,6 +61,13 @@
         @pl.when(exists[side])
         def _(side=side):
             pl.semaphore_signal(barrier, inc=1, device_id=peer(side), device_id_type=MESH)
+
+    fields = ((tracer, level0), (flow_j, flows.at[0]), (flow_i, flows.at[1]))
+    for number, some, spans in ((0, fields[:1], ((0, 2), (J - 2, 2))), (1, fields[1:], ((0, 2), (J - 2, 2))),
+                                (2, fields[:1], ((2, J - 4),)), (3, fields[1:], ((2, J - 4),))):
+        for src, dst in some:
+            for row, rows in spans:
+                pltpu.make_async_copy(src.at[pl.ds(row, rows)], view(dst, row, rows, 0, I), load_sem.at[number]).start()
 
     stages, known = [], 1
     while known < souths - 1:
@@ -98,9 +99,13 @@
         clear(level3, -2, 1, 0, I)
         clear(level3, J + 1, 1, 0, I)
         spill[...] = zeros(spill.shape)
-        for side, row in ((LOWER, -2), (UPPER, J)):
-            pl.when(jnp.logical_not(exists[side]))(lambda row=row: clear(level0, row, 2, -3, I + 6))
+        for side, row in ((LOWER, -1), (UPPER, J)):
+            pl.when(jnp.logical_not(exists[side]))(lambda row=row: clear(level0, row, 1, -3, I + 6))
         trim(0, 0, J, 4)
+        for side in (LEFT, RIGHT):
+            @pl.when(jnp.logical_not(exists[side]))
+            def _(side=side):
+                tracer_bits[side - LEFT, :, :, pl.ds((0, 2)[side - LEFT], 3), :] = zeros((2, 2, 3, M))
     with jax.named_scope("barw"):
         pl.semaphore_wait(barrier, near)
 
@@ -120,16 +125,20 @@
         return view(ref, row, rows, col, cols)
 
     def shift(side, ref, sems, *area):
-        return remote(side, block(ref, side, True, *area), block(ref, side, False, *area), send_sem.at[side], sems.at[side])
+        return remote(side, block(ref, side, True, *area), block(ref, side, False, *area), load_sem.at[side // 2], sems.at[side % (2 if sems is side_sem else 4)])
 
     def far_tracer(side):
-        return [shift(side, level0, far_sem, 0, 2, 0, I)]
-
-    def far_flows(side):
-        return [shift(side, flows, far_sem, 0, 1, 0, I)]
+        return [shift(side, level0, far_sem, 0, 1, 0, I)]
+
+    def far_flow(side):
+        return [shift(side, flows.at[0], far_sem, 0, 1, 0, I)]
+
+    def far_part(side):
+        area = pl.ds(TILE + 1, I - 2)
+        return [remote(side, mine.at[side, area, :], part.at[BACK[side], area, :], load_sem.at[side // 2], far_sem.at[side])]
 
     def far_last(side):
-        return [shift(side, flows.at[0], last_sem, 1, 1, 0, I)]
+        return [shift(side, flows.at[1], last_sem, 0, 1, 0, I), shift(side, flows.at[0], last_sem, 1, 1, 0, I)]
 
     def side_tracer(side):
         return [shift(side, level0, side_sem, 0, J, 0, 4)]
@@ -139,37 +148,58 @@
 
     bands = (LOWER, UPPER)
 
+    edge, nearest = (0, J - 1), (0, 1)
+
     def bits(side):
         out = []
+        to = BACK[side] - LEFT
         for band in bands:
-            at = {LEFT: 0, RIGHT: I - 3}[side], {LEFT: 0, RIGHT: I - 2}[side]
-            to = BACK[side] - LEFT
-            out += [remote(side, view(level0, (0, J - 2)[band], 2, at[0], 3), tracer_bits.at[to, band, :, pl.ds(0, 3), :],
-                           send_sem.at[side], bits_sem.at[to]),
-                    remote(side, flows.at[:, pl.ds((0, J - 1)[band] + PAD, 1), pl.ds(at[1] + TILE, 2), :],
-                           flow_bits.at[to, band, :, :, pl.ds(0, 2), :], send_sem.at[side], bits_sem.at[to])]
+            three, two = {LEFT: (0, 0), RIGHT: (I - 3, I - 2)}[side]
+            out += [remote(side, view(level0, (0, J - 2)[band], 2, three, 3),
+                           tracer_bits.at[to, band, :, pl.ds((0, 2)[to], 3), :], load_sem.at[side // 2], bits_sem.at[to]),
+                    remote(side, flows.at[:, edge[band] + PAD, pl.ds(two + TILE, 2), :],
+                           flow_bits.at[to, band, :, pl.ds((0, 1)[to], 2), :], load_sem.at[side // 2], bits_sem.at[to])]
         return out
 
-    def relay(band, side, here):
+    def own_bits():
+        for to, own_tracer, own_flow in ((0, (3, 0), (2, 0)), (1, (0, I - 2), (0, I - 1))):
+            for band in bands:
+                tracer_bits[to, band, :, pl.ds(own_tracer[0], 2), :] = view(level0, (0, J - 2)[band], 2, own_tracer[1], 2)[...]
+                flow_bits[to, band, :, pl.ds(own_flow[0], 1), :] = flows[:, edge[band] + PAD, pl.ds(own_flow[1] + TILE, 1), :]
+
+    def lone(band, middle, inside, left, right, flow_j, flow_i):
+        none = jnp.zeros_like(middle)
+        lower, upper = (none, inside) if band == LOWER else (inside, none)
+        return step(middle, lower, upper, left, right, flow_j, flow_i)
+
+    def relay(band, side):
         to = side - LEFT
-        row = (J, -2)[band], (J, -1)[band]
-        col = {LEFT: -3, RIGHT: I}[side], {LEFT: -2, RIGHT: I}[side]
-        src = ((tracer_bits.at[to, band, :, pl.ds(0, 3), :], flow_bits.at[to, band, :, :, pl.ds(0, 2), :]) if here else
-               (view(level0, (0, J - 2)[band], 2, col[0], 3),
-                flows.at[:, pl.ds((0, J - 1)[band] + PAD, 1), pl.ds(col[1] + TILE, 2), :]))
-        dst = (view(level0, row[0], 2, col[0], 3), flows.at[:, pl.ds(row[1] + PAD, 1), pl.ds(col[1] + TILE, 2), :])
-        return [remote(band, a, b, send_sem.at[band], far_sem.at[band]) for a, b in zip(src, dst)]
+        row = (J, -1)[band] + PAD
+        three, two, one, parts = ((-3, -2, -1, -2), (I, I, I, I - 1))[to]
+
+        def cells(src, dst, sem):
+            return remote(band, src, dst, load_sem.at[0], sem.at[band])
+
+        return [cells(tracer_bits.at[to, band, nearest[band], pl.ds((0, 2)[to], 3), :],
+                      level0.at[row, pl.ds(three + TILE, 3), :], far_sem),
+                cells(mine_bits.at[to, band, pl.ds(0, 3), :], part.at[BACK[band], pl.ds(parts + TILE, 3), :], far_sem),
+                cells(flow_bits.at[to, band, 0, pl.ds((0, 1)[to], 2), :], flows.at[0, row, pl.ds(two + TILE, 2), :], far_sem),
+                cells(flow_bits.at[to, band, 1, pl.ds(1, 1), :], flows.at[1, row, pl.ds(one + TILE, 1), :], last_sem)]
 
     def second(side):
         row = {LOWER: 0, UPPER: J - 2}[side]
         return remote(side, view(level2, row, 2, -1, I + 2), halo.at[BACK[side], :, pl.ds(TILE - 1, I + 2), :],
-                      late_sem.at[side], step_sem.at[side])
+                      load_sem.at[0], step_sem.at[side])
 
     def start(side, make):
         @pl.when(exists[side])
         def _():
             for copy in make():
                 copy.start()
+
+    def count(sem, cells):
+        area = tally.at[pl.ds(0, cells)]
+        pltpu.make_async_copy(area, area, sem).wait()
 
     def drain(sem, rows, cols, ref=None):
         part = (level0 if ref is None else ref).at[..., pl.ds(0, rows), pl.ds(0, cols), :]
@@ -199,16 +229,20 @@
                     start(side, lambda side=side: [copy for make in makes for copy in make(side)])
 
     def share(side):
-        for here in (True, False):
-            @pl.when(exists[side] if here else jnp.logical_not(exists[side]))
-            def _(here=here):
-                if here:
-                    drain(bits_sem.at[side - LEFT], 5, 4)
-                for band in bands:
-                    start(band, lambda band=band: relay(band, side, here))
+        to = side - LEFT
+        pl.when(exists[side])(lambda: count(bits_sem.at[to], 20))
+        for band in bands:
+            def at(near, col):
+                return tracer_bits[to, band, nearest[band] if near else 1 - nearest[band], pl.ds(col, 3), :]
+
+            mine_bits[to, band, pl.ds(0, 3), :] = lone(band, at(True, 1), at(False, 1), at(True, 0), at(True, 2),
+                                                       flow_bits[to, band, 0, pl.ds(0, 3), :],
+                                                       flow_bits[to, band, 1, pl.ds(0, 3), :])
+        for band in bands:
+            start(band, lambda band=band: relay(band, side))
 
     def strip(side):
-        pl.when(exists[side])(lambda: drain(side_sem.at[BACK[side]], J, 10))
+        pl.when(exists[side])(lambda: drain(side_sem.at[BACK[side] % 2], J, 10))
         for k in range(1, 5):
             sweep(k, k, J - k, {LEFT: k - 4, RIGHT: I - k}[side], 4, 15)
             if k < 4:
@@ -219,9 +253,16 @@
         both(far_tracer)
     with jax.named_scope("load1"):
         drain(load_sem.at[1], 4, I, flows)
-        both(far_flows)
         for side in (LEFT, RIGHT):
             start(side, lambda side=side: bits(side))
+        both(far_flow)
+        for band in bands:
+            row, inside = edge[band], (1, J - 2)[band]
+            mine[band, pl.ds(TILE + 1, I - 2), :] = lone(
+                band, *(line(level0, r, c, I - 2) for r, c in ((row, 1), (inside, 1), (row, 0), (row, 2))),
+                *(line(flows.at[k], row, 1, I - 2) for k in (0, 1)))
+        own_bits()
+        both(far_part)
         if stages:
             tell(0)
     with jax.named_scope("load2"):
@@ -240,14 +281,15 @@
         def _(early=early, late=late):
             with jax.named_scope("early"):
                 share(early)
+                pl.when(jnp.logical_not(exists[late]))(lambda: share(late))
+                strip(early)
                 both(far_last)
-                strip(early)
             with jax.named_scope("hear0"):
                 for stage in range(1, len(stages) - 1):
                     hear(stage - 1)
                     tell(stage)
             with jax.named_scope("share"):
-                share(late)
+                pl.when(exists[late])(lambda: share(late))
             with jax.named_scope("hear1"):
                 for stage in range(max(1, len(stages) - 1), len(stages)):
                     hear(stage - 1)
@@ -260,11 +302,12 @@
 
     with jax.named_scope("recvj"):
         for side in (LOWER, UPPER):
-            pl.when(exists[side])(lambda side=side: drain(far_sem.at[BACK[side]], 4, I + 5))
+            pl.when(exists[side])(lambda side=side: count(far_sem.at[BACK[side]], 3 * I + 14))
     with jax.named_scope("rim2"):
-        for inner, outer in ((0, -1), (J - 1, J)):
+        for side, inner, outer, sign in ((LOWER, 0, -1, -1.0), (UPPER, J - 1, J, 1.0)):
             update(1, inner, 1, -3, I + 6)
-            update(1, outer, 1, -2, I + 4)
+            level1[outer + PAD, pl.ds(TILE - 2, I + 4), :] = part[side, pl.ds(TILE - 2, I + 4), :] + (
+                RATE + sign * line(flows.at[0], outer, -2, I + 4)) * line(level0, inner, -2, I + 4)
             trim(1, inner, 1, 3)
             trim(1, outer, 1, 2)
         for side, outer in ((LOWER, -1), (UPPER, J)):
@@ -274,19 +317,26 @@
             trim(2, row, 2, 2)
             start(side, lambda side=side: [second(side)])
     with jax.named_scope("rim4"):
-        for side in (LOWER, UPPER):
-            pl.when(exists[side])(lambda side=side: drain(last_sem.at[BACK[side]], 1, I))
-        for side, row, outer in ((LOWER, -1, -1), (UPPER, J - 3, J)):
-            update(3, row, 4, -1, I + 2)
-            trim(3, row, 4, 1)
-            pl.when(jnp.logical_not(exists[side]))(lambda outer=outer: clear(level3, outer, 1, -1, I + 2))
-        for side, row, outer, last, sign in ((LOWER, 0, -1, -2, -1.0), (UPPER, J - 4, J, J + 1, 1.0)):
+        for side, edge_row, outer, three, sign in ((LOWER, 0, -1, 0, -1.0), (UPPER, J - 1, J, J - 3, 1.0)):
+            update(3, three, 3, -1, I + 2)
+            trim(3, three, 3, 1)
+            level3[outer + PAD, pl.ds(TILE - 1, I + 2), :] = zeros((I + 2, M))
+
+            @pl.when(exists[side])
+            def _(edge_row=edge_row, outer=outer, sign=sign):
+                level3[outer + PAD, pl.ds(TILE - 1, I + 2), :] = (
+                    RATE + sign * line(flows.at[0], outer, -1, I + 2)) * line(level2, edge_row, -1, I + 2)
+
+            trim(3, outer, 1, 1)
+        for row in (0, J - 4):
             update(4, row, 4, 0, I)
             for r in range(4):
                 total = total + end[row + r]
-
+    with jax.named_scope("spill"):
+        for side, outer, last, sign in ((LOWER, -1, -2, -1.0), (UPPER, J, J + 1, 1.0)):
             @pl.when(exists[side])
             def _(side=side, outer=outer, last=last, sign=sign):
+                count(last_sem.at[BACK[side]], 2 * I + 2)
                 value = advance(level3, flows, outer, 1, 0, I)[0]
                 spill[side] = value + (RATE + sign * line(flows.at[0], last, 0, I)) * line(level3, outer, 0, I)
 
@@ -294,7 +344,7 @@
 
     def total_copy(source, other):
         return pltpu.make_async_remote_copy(
-            src_ref=own, dst_ref=totals.at[source], send_sem=total_send, recv_sem=total_recv,
+            src_ref=own, dst_ref=totals.at[source], send_sem=load_sem.at[2], recv_sem=total_recv,
             device_id={"south": other, "east": e}, device_id_type=MESH)
 
     with jax.named_scope("give"):
@@ -342,19 +392,18 @@
                     spill[LOWER] = spill[LOWER] - first - then
 
     with jax.named_scope("sent"):
-        for side in range(4):
-            rows, cols = (5, I + 4) if side in (LOWER, UPPER) else (J + 2, 10)
-            pl.when(exists[side])(lambda side=side, rows=rows, cols=cols: drain(send_sem.at[side], rows, cols))
-        for side in (LOWER, UPPER):
-            pl.when(exists[side])(lambda side=side: second(side).wait_send())
+        for kind, sides, cells in ((0, (LOWER, UPPER), 7 * I + 20), (1, (LEFT, RIGHT), 10 * (J + 2))):
+            one, two = (exists[side] for side in sides)
+            pl.when(one != two)(lambda kind=kind, cells=cells: count(load_sem.at[kind], cells))
+            pl.when(one & two)(lambda kind=kind, cells=cells: count(load_sem.at[kind], 2 * cells))
     with jax.named_scope("take"):
-        for count in range(1, souths):
-            part = totals.at[pl.ds(0, count)]
-            pl.when(s == count)(lambda part=part: pltpu.make_async_copy(part, part, total_recv).wait())
+        for given in range(1, souths):
+            piece = totals.at[pl.ds(0, given)]
+            pl.when(s == given)(lambda piece=piece: pltpu.make_async_copy(piece, piece, total_recv).wait())
         before[...] = lax.fori_loop(0, s, lambda source, state: state + totals[source], spill[LOWER])
-    for count in range(1, souths):
-        part = totals.at[pl.ds(0, count)]
-        pl.when(s == souths - 1 - count)(lambda part=part: pltpu.make_async_copy(part, part, total_send).wait())
+    for given in range(1, souths):
+        piece = totals.at[pl.ds(0, given)]
+        pl.when(s == souths - 1 - given)(lambda piece=piece: pltpu.make_async_copy(piece, piece, load_sem.at[2]).wait())
 
 
 def write_out(scale, before, end, running_out, end_out, running, sems):
@@ -391,12 +440,16 @@
             pltpu.VMEM((2, 2) + padded[1:], jnp.float32),
             pltpu.VMEM((2,) + padded[1:], jnp.float32),
             pltpu.VMEM((2, I, M), jnp.float32),
+            pltpu.VMEM((2,) + padded[1:], jnp.float32),
             pltpu.VMEM((2, 2, 2, TILE, M), jnp.float32),
-            pltpu.VMEM((2, 2, 2, 1, TILE, M), jnp.float32),
+            pltpu.VMEM((2, 2, 2, TILE, M), jnp.float32),
+            pltpu.VMEM((2,) + padded[1:], jnp.float32),
+            pltpu.VMEM((2, 2, TILE, M), jnp.float32),
+            pltpu.VMEM((max(20 * (J + 2), 14 * I + 40), M), jnp.float32),
             pltpu.VMEM((I, M), jnp.float32),
             pltpu.VMEM((souths, I, M), jnp.float32),
             pltpu.SemaphoreType.REGULAR((max(1, (souths - 1).bit_length()),)),
-            dma((4,)), dma((4,)), dma((2,)), dma((2,)), dma((4,)), dma((2,)), dma((2,)), dma((2,)), dma, dma,
+            dma((4,)), dma((2,)), dma((2,)), dma((2,)), dma((2,)), dma((2,)), dma,
         ],
         compiler_params=pltpu.CompilerParams(collective_id=0, has_side_effects=True,
                                              vmem_limit_bytes=106 * 2 ** 19),

time: 14.8 us -> 14.4 us (0.973)
  the two profiles are of different devices: /device:TPU:24 before, /device:TPU:25 now
where the time goes in v2:
time: 14.4 us; the launch traced here: 14.3 us
  Pallas kernels  13.6 us (94%)
  between operations  0.64 us (4%)
    pallas_call x1, Pallas kernels, per_device(): pl.pallas_call(functools.partial(kernel, souths, easts), out_shape=(jax.S...  12.6 us
    pallas_call x1, Pallas kernels, per_device(): pl.pallas_call(functools.partial(write_out, 1.0 / (J * souths)), out_shap...  0.99 us

profile of v2, /device:TPU:25, one launch (start us, length us, event | category | flops | bytes accessed | tf_op | source)
XLA Modules:
  0.0 14.3 jit_solution(3680303594524181011)
XLA Ops:
  0.6 12.6 %shard_map.50 = (f32[32,128]{1,0:T(8,128)S(1)}, f32[32,32,128]{2,1,0:T(8,128)S(1)}) custom-call(f32[32,32,128]{2,1,0:T(8,128)} %tracer.1, f32[32,32,128]{2,1,0:T(8,128)} %flow_j.1, f32[32,32,128]{2,1,0:T(8,128)} %flow_i.1), custom_call_target="tpu_custom_call" | custom-call | tf_op jit(solution)/shard_map/pallas_call | solution.py:432
  13.3 1.0 %shard_map.51 = (f32[32,32,128]{2,1,0:T(8,128)}, f32[32,32,128]{2,1,0:T(8,128)}) custom-call(f32[32,128]{1,0:T(8,128)S(1)} %get-tuple-element.4.before, f32[32,32,128]{2,1,0:T(8,128)S(1)} %get-tuple-element.5.end), custom_call_target="tpu_custom_call" | custom-call | tf_op jit(solution)/shard_map/pallas_call | solution.py:457

commit v3 on v2

--- a/solution.py
+++ b/solution.py
@@ -283,13 +283,13 @@
                 share(early)
                 pl.when(jnp.logical_not(exists[late]))(lambda: share(late))
                 strip(early)
-                both(far_last)
             with jax.named_scope("hear0"):
                 for stage in range(1, len(stages) - 1):
                     hear(stage - 1)
                     tell(stage)
             with jax.named_scope("share"):
                 pl.when(exists[late])(lambda: share(late))
+                both(far_last)
             with jax.named_scope("hear1"):
                 for stage in range(max(1, len(stages) - 1), len(stages)):
                     hear(stage - 1)
@@ -351,11 +351,12 @@
         if stages:
             hear(len(stages) - 1)
 
-        def give(turn, _):
-            total_copy(s, s + turn).start()
-            return 0
-
-        lax.fori_loop(1, souths - s, give, 0)
+        def give(first, turn):
+            total_copy(s, s + first + 2 * turn).start()
+            return first
+
+        for first in (1, 2):
+            lax.fori_loop(0, (souths - s + 1 - first) // 2, lambda turn, _, first=first: give(first, turn), first)
 
     with jax.named_scope("recv2"):
         for side in (LOWER, UPPER):

time: 14.4 us -> 14 us (0.972)
  Pallas kernels: 13.6 us -> 13.2 us
    pallas_call x1, Pallas kernels: 12.6 us -> 12.2 us  [per_device(): pl.pallas_call(functools.partial(kernel, souths, easts), out_shape=(jax.S...]
where the time goes in v3:
time: 14 us; the launch traced here: 13.9 us
  Pallas kernels  13.2 us (94%)
  between operations  0.64 us (5%)
    pallas_call x1, Pallas kernels, per_device(): pl.pallas_call(functools.partial(kernel, souths, easts), out_shape=(jax.S...  12.2 us
    pallas_call x1, Pallas kernels, per_device(): pl.pallas_call(functools.partial(write_out, 1.0 / (J * souths)), out_shap...  0.99 us

profile of v3, /device:TPU:25, one launch (start us, length us, event | category | flops | bytes accessed | tf_op | source)
XLA Modules:
  0.0 13.9 jit_solution(6074454240817381107)
XLA Ops:
  0.6 12.2 %shard_map.50 = (f32[32,128]{1,0:T(8,128)S(1)}, f32[32,32,128]{2,1,0:T(8,128)S(1)}) custom-call(f32[32,32,128]{2,1,0:T(8,128)} %tracer.1, f32[32,32,128]{2,1,0:T(8,128)} %flow_j.1, f32[32,32,128]{2,1,0:T(8,128)} %flow_i.1), custom_call_target="tpu_custom_call" | custom-call | tf_op jit(solution)/shard_map/pallas_call | solution.py:433
  12.9 1.0 %shard_map.51 = (f32[32,32,128]{2,1,0:T(8,128)}, f32[32,32,128]{2,1,0:T(8,128)}) custom-call(f32[32,128]{1,0:T(8,128)S(1)} %get-tuple-element.4.before, f32[32,32,128]{2,1,0:T(8,128)S(1)} %get-tuple-element.5.end), custom_call_target="tpu_custom_call" | custom-call | tf_op jit(solution)/shard_map/pallas_call | solution.py:458

commit v4 on v2

--- a/solution.py
+++ b/solution.py
@@ -43,7 +43,7 @@
 
 def kernel(souths, easts, tracer, flow_j, flow_i, before, end, level0, level1, level2, level3, flows, halo, reply, spill,
            part, tracer_bits, flow_bits, mine, mine_bits, tally, own, totals, ready, load_sem, bits_sem, side_sem, far_sem, last_sem,
-           step_sem, total_recv):
+           step_sem, total_recv, diag_sem, greeted):
     J, I, M = tracer.shape
     s, e = lax.axis_index("south"), lax.axis_index("east")
     levels = (level0, level1, level2, level3)
@@ -108,6 +108,11 @@
                 tracer_bits[side - LEFT, :, :, pl.ds((0, 2)[side - LEFT], 3), :] = zeros((2, 2, 3, M))
     with jax.named_scope("barw"):
         pl.semaphore_wait(barrier, near)
+        for turn, late in enumerate((LEFT, RIGHT)):
+            @pl.when((lax.rem(e, 2) == turn) & exists[late])
+            def _(late=late):
+                pl.semaphore_signal(greeted, inc=1, device_id=peer(late), device_id_type=MESH)
+    later = ((lax.rem(e, 2) == 0) & exists[LEFT]) | ((lax.rem(e, 2) == 1) & exists[RIGHT])
 
     def remote(side, src, dst, send, recv):
         return pltpu.make_async_remote_copy(src_ref=src, dst_ref=dst, send_sem=send, recv_sem=recv,
@@ -175,7 +180,7 @@
     def relay(band, side):
         to = side - LEFT
         row = (J, -1)[band] + PAD
-        three, two, one, parts = ((-3, -2, -1, -2), (I, I, I, I - 1))[to]
+        three, two, parts = ((-3, -2, -2), (I, I, I - 1))[to]
 
         def cells(src, dst, sem):
             return remote(band, src, dst, load_sem.at[0], sem.at[band])
@@ -183,8 +188,26 @@
         return [cells(tracer_bits.at[to, band, nearest[band], pl.ds((0, 2)[to], 3), :],
                       level0.at[row, pl.ds(three + TILE, 3), :], far_sem),
                 cells(mine_bits.at[to, band, pl.ds(0, 3), :], part.at[BACK[band], pl.ds(parts + TILE, 3), :], far_sem),
-                cells(flow_bits.at[to, band, 0, pl.ds((0, 1)[to], 2), :], flows.at[0, row, pl.ds(two + TILE, 2), :], far_sem),
-                cells(flow_bits.at[to, band, 1, pl.ds(1, 1), :], flows.at[1, row, pl.ds(one + TILE, 1), :], last_sem)]
+                cells(flow_bits.at[to, band, 0, pl.ds((0, 1)[to], 2), :], flows.at[0, row, pl.ds(two + TILE, 2), :], far_sem)]
+
+    def cell(band, side):
+        area = pl.ds({LEFT: 0, RIGHT: I - 1}[side] + TILE, 1)
+        row = (J + 1, -2)[band] + PAD
+        return [remote(band, level0.at[(1, J - 2)[band] + PAD, area, :], level0.at[row, area, :], load_sem.at[0], far_sem.at[band]),
+                remote(band, flows.at[1, edge[band] + PAD, area, :], flows.at[1, row, area, :], load_sem.at[0], far_sem.at[band])]
+
+    def diagonal(band, side):
+        row = (J, -1)[band] + PAD, (J + 1, -2)[band] + PAD
+        home, away = {LEFT: ((0, 0), (I, I)), RIGHT: ((I - 3, I - 2), (-3, -2))}[side]
+
+        def cells(src, dst):
+            return pltpu.make_async_remote_copy(
+                src_ref=src, dst_ref=dst, send_sem=load_sem.at[3], recv_sem=diag_sem.at[band],
+                device_id={"south": s + SIDES[band][0], "east": e + SIDES[side][1]}, device_id_type=MESH)
+
+        return [cells(view(level0, (0, J - 2)[band], 2, home[0], 3), view(level0, (J, -2)[band], 2, away[0], 3))] + [
+            cells(flows.at[k, edge[band] + PAD, pl.ds(home[1] + TILE, 2), :], flows.at[k, row[k], pl.ds(away[1] + TILE, 2), :])
+            for k in (0, 1)]
 
     def second(side):
         row = {LOWER: 0, UPPER: J - 2}[side]
@@ -253,8 +276,15 @@
         both(far_tracer)
     with jax.named_scope("load1"):
         drain(load_sem.at[1], 4, I, flows)
-        for side in (LEFT, RIGHT):
-            start(side, lambda side=side: bits(side))
+        for turn, (early, late) in enumerate(((RIGHT, LEFT), (LEFT, RIGHT))):
+            @pl.when(lax.rem(e, 2) == turn)
+            def _(early=early, late=late):
+                start(early, lambda: bits(early))
+
+                @pl.when(exists[late])
+                def _():
+                    for band in bands:
+                        start(band, lambda band=band: cell(band, late))
         both(far_flow)
         for band in bands:
             row, inside = edge[band], (1, J - 2)[band]
@@ -276,20 +306,29 @@
     with jax.named_scope("inner"):
         for k in range(1, 5):
             sweep(k, k, J - k, k, I - 2 * k, 7)
+    def greet():
+        for stage in range(1, len(stages) - 1):
+            hear(stage - 1)
+            tell(stage)
+
     for turn, (early, late) in enumerate(((RIGHT, LEFT), (LEFT, RIGHT))):
         @pl.when(lax.rem(e, 2) == turn)
         def _(early=early, late=late):
+            with jax.named_scope("diag"):
+                @pl.when(exists[late])
+                def _():
+                    pl.semaphore_wait(greeted, 1)
+                    for band in bands:
+                        start(band, lambda band=band: diagonal(band, late))
+            with jax.named_scope("hearx"):
+                pl.when(2 * e >= easts)(greet)
             with jax.named_scope("early"):
                 share(early)
                 pl.when(jnp.logical_not(exists[late]))(lambda: share(late))
                 strip(early)
                 both(far_last)
             with jax.named_scope("hear0"):
-                for stage in range(1, len(stages) - 1):
-                    hear(stage - 1)
-                    tell(stage)
-            with jax.named_scope("share"):
-                pl.when(exists[late])(lambda: share(late))
+                pl.when(2 * e < easts)(greet)
             with jax.named_scope("hear1"):
                 for stage in range(max(1, len(stages) - 1), len(stages)):
                     hear(stage - 1)
@@ -300,43 +339,56 @@
     for row in range(5, J - 4):
         total = total + end[row]
 
-    with jax.named_scope("recvj"):
-        for side in (LOWER, UPPER):
-            pl.when(exists[side])(lambda side=side: count(far_sem.at[BACK[side]], 3 * I + 14))
-    with jax.named_scope("rim2"):
-        for side, inner, outer, sign in ((LOWER, 0, -1, -1.0), (UPPER, J - 1, J, 1.0)):
-            update(1, inner, 1, -3, I + 6)
-            level1[outer + PAD, pl.ds(TILE - 2, I + 4), :] = part[side, pl.ds(TILE - 2, I + 4), :] + (
-                RATE + sign * line(flows.at[0], outer, -2, I + 4)) * line(level0, inner, -2, I + 4)
-            trim(1, inner, 1, 3)
-            trim(1, outer, 1, 2)
-        for side, outer in ((LOWER, -1), (UPPER, J)):
-            pl.when(jnp.logical_not(exists[side]))(lambda outer=outer: clear(level1, outer, 1, -2, I + 4))
-        for side, row in ((LOWER, 0), (UPPER, J - 2)):
-            update(2, row, 2, -2, I + 4)
-            trim(2, row, 2, 2)
-            start(side, lambda side=side: [second(side)])
-    with jax.named_scope("rim4"):
-        for side, edge_row, outer, three, sign in ((LOWER, 0, -1, 0, -1.0), (UPPER, J - 1, J, J - 3, 1.0)):
-            update(3, three, 3, -1, I + 2)
-            trim(3, three, 3, 1)
-            level3[outer + PAD, pl.ds(TILE - 1, I + 2), :] = zeros((I + 2, M))
-
-            @pl.when(exists[side])
-            def _(edge_row=edge_row, outer=outer, sign=sign):
-                level3[outer + PAD, pl.ds(TILE - 1, I + 2), :] = (
-                    RATE + sign * line(flows.at[0], outer, -1, I + 2)) * line(level2, edge_row, -1, I + 2)
-
-            trim(3, outer, 1, 1)
-        for row in (0, J - 4):
-            update(4, row, 4, 0, I)
-            for r in range(4):
-                total = total + end[row + r]
+    def rim(side):
+        edge_row, outer, two, three, four, sign = ((0, -1, 0, 0, 0, -1.0), (J - 1, J, J - 2, J - 3, J - 4, 1.0))[side]
+        pl.when(exists[side] & jnp.logical_not(later))(lambda: count(far_sem.at[BACK[side]], 3 * I + 14))
+
+        @pl.when(exists[side] & later)
+        def _():
+            count(far_sem.at[BACK[side]], 3 * I + 8)
+            count(diag_sem.at[BACK[side]], 10)
+        beyond = outer + outer - edge_row
+        for turn, col in enumerate((-2, I - 1)):
+            @pl.when((lax.rem(e, 2) == turn) & exists[side] & later)
+            def _(col=col):
+                part[side, pl.ds(TILE + col, 3), :] = lone(
+                    BACK[side], *(line(level0, r, c, 3) for r, c in
+                                  ((outer, col), (beyond, col), (outer, col - 1), (outer, col + 1))),
+                    line(flows.at[0], outer, col, 3), line(flows.at[1], beyond, col, 3))
+        update(1, edge_row, 1, -3, I + 6)
+        trim(1, edge_row, 1, 3)
+        level1[outer + PAD, pl.ds(TILE - 2, I + 4), :] = part[side, pl.ds(TILE - 2, I + 4), :] + (
+            RATE + sign * line(flows.at[0], outer, -2, I + 4)) * line(level0, edge_row, -2, I + 4)
+        trim(1, outer, 1, 2)
+        pl.when(jnp.logical_not(exists[side]))(lambda: clear(level1, outer, 1, -2, I + 4))
+        update(2, two, 2, -2, I + 4)
+        trim(2, two, 2, 2)
+        start(side, lambda: [second(side)])
+        update(3, three, 3, -1, I + 2)
+        trim(3, three, 3, 1)
+        level3[outer + PAD, pl.ds(TILE - 1, I + 2), :] = zeros((I + 2, M))
+
+        @pl.when(exists[side])
+        def _():
+            level3[outer + PAD, pl.ds(TILE - 1, I + 2), :] = (
+                RATE + sign * line(flows.at[0], outer, -1, I + 2)) * line(level2, edge_row, -1, I + 2)
+
+        trim(3, outer, 1, 1)
+        update(4, four, 4, 0, I)
+
+    for turn, sides in enumerate(((LOWER, UPPER), (UPPER, LOWER))):
+        @pl.when(lax.rem(s, 2) == turn)
+        def _(sides=sides):
+            for number, side in enumerate(sides):
+                with jax.named_scope(f"rim{number}"):
+                    rim(side)
+    for row in (*range(4), *range(J - 4, J)):
+        total = total + end[row]
     with jax.named_scope("spill"):
         for side, outer, last, sign in ((LOWER, -1, -2, -1.0), (UPPER, J, J + 1, 1.0)):
             @pl.when(exists[side])
             def _(side=side, outer=outer, last=last, sign=sign):
-                count(last_sem.at[BACK[side]], 2 * I + 2)
+                count(last_sem.at[BACK[side]], 2 * I)
                 value = advance(level3, flows, outer, 1, 0, I)[0]
                 spill[side] = value + (RATE + sign * line(flows.at[0], last, 0, I)) * line(level3, outer, 0, I)
 
@@ -348,14 +400,22 @@
             device_id={"south": other, "east": e}, device_id_type=MESH)
 
     with jax.named_scope("give"):
+        def give(first, lower, upper):
+            def one(turn, _):
+                total_copy(s, s + first + 2 * turn).start()
+                return 0
+
+            lax.fori_loop(lower, upper, one, 0)
+
+        reach = stages[-1] if stages else souths
+        for first in (1, 2):
+            most = (souths - s + 1 - first) // 2
+            give(first, 0, jnp.minimum(most, (reach + 2 - first) // 2))
         if stages:
             hear(len(stages) - 1)
-
-        def give(turn, _):
-            total_copy(s, s + turn).start()
-            return 0
-
-        lax.fori_loop(1, souths - s, give, 0)
+            for first in (1, 2):
+                most, done = (souths - s + 1 - first) // 2, (reach + 2 - first) // 2
+                give(first, jnp.minimum(most, done), most)
 
     with jax.named_scope("recv2"):
         for side in (LOWER, UPPER):
@@ -392,10 +452,18 @@
                     spill[LOWER] = spill[LOWER] - first - then
 
     with jax.named_scope("sent"):
-        for kind, sides, cells in ((0, (LOWER, UPPER), 7 * I + 20), (1, (LEFT, RIGHT), 10 * (J + 2))):
-            one, two = (exists[side] for side in sides)
-            pl.when(one != two)(lambda kind=kind, cells=cells: count(load_sem.at[kind], cells))
-            pl.when(one & two)(lambda kind=kind, cells=cells: count(load_sem.at[kind], 2 * cells))
+        one, two = exists[LOWER], exists[UPPER]
+        for has, cells, slanted in ((later, 7 * I + 12, 10), (jnp.logical_not(later), 7 * I + 18, 0)):
+            for many, number in ((one != two, 1), (one & two, 2)):
+                @pl.when(has & many)
+                def _(cells=cells, slanted=slanted, number=number):
+                    count(load_sem.at[0], number * cells)
+                    if slanted:
+                        count(load_sem.at[3], number * slanted)
+        sooner = ((lax.rem(e, 2) == 0) & exists[RIGHT]) | ((lax.rem(e, 2) == 1) & exists[LEFT])
+        pl.when(sooner & later)(lambda: count(load_sem.at[1], 20 * (J + 1)))
+        pl.when(sooner & jnp.logical_not(later))(lambda: count(load_sem.at[1], 10 * (J + 2)))
+        pl.when(later & jnp.logical_not(sooner))(lambda: count(load_sem.at[1], 10 * J))
     with jax.named_scope("take"):
         for given in range(1, souths):
             piece = totals.at[pl.ds(0, given)]
@@ -449,7 +517,7 @@
             pltpu.VMEM((I, M), jnp.float32),
             pltpu.VMEM((souths, I, M), jnp.float32),
             pltpu.SemaphoreType.REGULAR((max(1, (souths - 1).bit_length()),)),
-            dma((4,)), dma((2,)), dma((2,)), dma((2,)), dma((2,)), dma((2,)), dma,
+            dma((4,)), dma((2,)), dma((2,)), dma((2,)), dma((2,)), dma((2,)), dma, dma((2,)), pltpu.SemaphoreType.REGULAR,
         ],
         compiler_params=pltpu.CompilerParams(collective_id=0, has_side_effects=True,
                                              vmem_limit_bytes=106 * 2 ** 19),

time: 14.4 us -> 13.9 us (0.965)
  the two profiles are of different devices: /device:TPU:25 before, /device:TPU:24 now
where the time goes in v4:
time: 13.9 us; the launch traced here: 13.6 us
  Pallas kernels  13 us (94%)
  between operations  0.64 us (5%)
    pallas_call x1, Pallas kernels, per_device(): pl.pallas_call(functools.partial(kernel, souths, easts), out_shape=(jax.S...  12 us
    pallas_call x1, Pallas kernels, per_device(): pl.pallas_call(functools.partial(write_out, 1.0 / (J * souths)), out_shap...  0.99 us

profile of v4, /device:TPU:24, one launch (start us, length us, event | category | flops | bytes accessed | tf_op | source)
XLA Modules:
  0.0 13.6 jit_solution(16202387795433291830)
XLA Ops:
  0.6 12.0 %shard_map.50 = (f32[32,128]{1,0:T(8,128)S(1)}, f32[32,32,128]{2,1,0:T(8,128)S(1)}) custom-call(f32[32,32,128]{2,1,0:T(8,128)} %tracer.1, f32[32,32,128]{2,1,0:T(8,128)} %flow_j.1, f32[32,32,128]{2,1,0:T(8,128)} %flow_i.1), custom_call_target="tpu_custom_call" | custom-call | tf_op jit(solution)/shard_map/pallas_call | solution.py:500
  12.6 1.0 %shard_map.51 = (f32[32,32,128]{2,1,0:T(8,128)}, f32[32,32,128]{2,1,0:T(8,128)}) custom-call(f32[32,128]{1,0:T(8,128)S(1)} %get-tuple-element.4.before, f32[32,32,128]{2,1,0:T(8,128)S(1)} %get-tuple-element.5.end), custom_call_target="tpu_custom_call" | custom-call | tf_op jit(solution)/shard_map/pallas_call | solution.py:525

commit v5 on v4

--- a/solution.py
+++ b/solution.py
@@ -400,22 +400,23 @@
             device_id={"south": other, "east": e}, device_id_type=MESH)
 
     with jax.named_scope("give"):
-        def give(first, lower, upper):
+        reach = stages[-1] if stages else souths
+        odd, even = (souths - s) // 2, (souths - s - 1) // 2
+        near_odd, near_even = jnp.minimum(odd, (reach + 1) // 2), jnp.minimum(even, reach // 2)
+
+        def give(lower, upper, distance):
             def one(turn, _):
-                total_copy(s, s + first + 2 * turn).start()
+                total_copy(s, s + distance(turn)).start()
                 return 0
 
             lax.fori_loop(lower, upper, one, 0)
 
-        reach = stages[-1] if stages else souths
-        for first in (1, 2):
-            most = (souths - s + 1 - first) // 2
-            give(first, 0, jnp.minimum(most, (reach + 2 - first) // 2))
+        give(0, near_odd, lambda turn: 2 * turn + 1)
+        give(0, near_even, lambda turn: 2 * (near_even - turn))
         if stages:
             hear(len(stages) - 1)
-            for first in (1, 2):
-                most, done = (souths - s + 1 - first) // 2, (reach + 2 - first) // 2
-                give(first, jnp.minimum(most, done), most)
+            give(near_odd, odd, lambda turn: 2 * turn + 1)
+            give(0, even - near_even, lambda turn: 2 * (even - turn))
 
     with jax.named_scope("recv2"):
         for side in (LOWER, UPPER):

time: 13.9 us -> 13.8 us (level)
  no operation moved by 1% of the time
where the time goes in v5:
time: 13.8 us; the launch traced here: 13.6 us
  Pallas kernels  13 us (94%)
  between operations  0.64 us (5%)
    pallas_call x1, Pallas kernels, per_device(): pl.pallas_call(functools.partial(kernel, souths, easts), out_shape=(jax.S...  12 us
    pallas_call x1, Pallas kernels, per_device(): pl.pallas_call(functools.partial(write_out, 1.0 / (J * souths)), out_shap...  0.99 us

profile of v5, /device:TPU:24, one launch (start us, length us, event | category | flops | bytes accessed | tf_op | source)
XLA Modules:
  0.0 13.6 jit_solution(1999563889258403413)
XLA Ops:
  0.6 12.0 %shard_map.50 = (f32[32,128]{1,0:T(8,128)S(1)}, f32[32,32,128]{2,1,0:T(8,128)S(1)}) custom-call(f32[32,32,128]{2,1,0:T(8,128)} %tracer.1, f32[32,32,128]{2,1,0:T(8,128)} %flow_j.1, f32[32,32,128]{2,1,0:T(8,128)} %flow_i.1), custom_call_target="tpu_custom_call" | custom-call | tf_op jit(solution)/shard_map/pallas_call | solution.py:501
  12.6 1.0 %shard_map.51 = (f32[32,32,128]{2,1,0:T(8,128)}, f32[32,32,128]{2,1,0:T(8,128)}) custom-call(f32[32,128]{1,0:T(8,128)S(1)} %get-tuple-element.4.before, f32[32,32,128]{2,1,0:T(8,128)S(1)} %get-tuple-element.5.end), custom_call_target="tpu_custom_call" | custom-call | tf_op jit(solution)/shard_map/pallas_call | solution.py:526

commit v6 on v5

--- a/solution.py
+++ b/solution.py
@@ -43,7 +43,7 @@
 
 def kernel(souths, easts, tracer, flow_j, flow_i, before, end, level0, level1, level2, level3, flows, halo, reply, spill,
            part, tracer_bits, flow_bits, mine, mine_bits, tally, own, totals, ready, load_sem, bits_sem, side_sem, far_sem, last_sem,
-           step_sem, total_recv, diag_sem, greeted):
+           step_sem, total_recv, greeted):
     J, I, M = tracer.shape
     s, e = lax.axis_index("south"), lax.axis_index("east")
     levels = (level0, level1, level2, level3)
@@ -161,9 +161,9 @@
         for band in bands:
             three, two = {LEFT: (0, 0), RIGHT: (I - 3, I - 2)}[side]
             out += [remote(side, view(level0, (0, J - 2)[band], 2, three, 3),
-                           tracer_bits.at[to, band, :, pl.ds((0, 2)[to], 3), :], load_sem.at[side // 2], bits_sem.at[to]),
+                           tracer_bits.at[to, band, :, pl.ds((0, 2)[to], 3), :], load_sem.at[side // 2], bits_sem),
                     remote(side, flows.at[:, edge[band] + PAD, pl.ds(two + TILE, 2), :],
-                           flow_bits.at[to, band, :, pl.ds((0, 1)[to], 2), :], load_sem.at[side // 2], bits_sem.at[to])]
+                           flow_bits.at[to, band, :, pl.ds((0, 1)[to], 2), :], load_sem.at[side // 2], bits_sem)]
         return out
 
     def own_bits():
@@ -202,7 +202,7 @@
 
         def cells(src, dst):
             return pltpu.make_async_remote_copy(
-                src_ref=src, dst_ref=dst, send_sem=load_sem.at[3], recv_sem=diag_sem.at[band],
+                src_ref=src, dst_ref=dst, send_sem=load_sem.at[3], recv_sem=far_sem.at[band],
                 device_id={"south": s + SIDES[band][0], "east": e + SIDES[side][1]}, device_id_type=MESH)
 
         return [cells(view(level0, (0, J - 2)[band], 2, home[0], 3), view(level0, (J, -2)[band], 2, away[0], 3))] + [
@@ -253,7 +253,7 @@
 
     def share(side):
         to = side - LEFT
-        pl.when(exists[side])(lambda: count(bits_sem.at[to], 20))
+        pl.when(exists[side])(lambda: count(bits_sem, 20))
         for band in bands:
             def at(near, col):
                 return tracer_bits[to, band, nearest[band] if near else 1 - nearest[band], pl.ds(col, 3), :]
@@ -345,8 +345,7 @@
 
         @pl.when(exists[side] & later)
         def _():
-            count(far_sem.at[BACK[side]], 3 * I + 8)
-            count(diag_sem.at[BACK[side]], 10)
+            count(far_sem.at[BACK[side]], 3 * I + 18)
         beyond = outer + outer - edge_row
         for turn, col in enumerate((-2, I - 1)):
             @pl.when((lax.rem(e, 2) == turn) & exists[side] & later)
@@ -477,7 +476,7 @@
 
 def write_out(scale, before, end, running_out, end_out, running, sems):
     J = end.shape[0]
-    parts = 2 if J % 2 == 0 else 1
+    parts = 1
     rows = J // parts
     copies = [pltpu.make_async_copy(end, end_out, sems.at[0])]
     copies[0].start()
@@ -518,7 +517,7 @@
             pltpu.VMEM((I, M), jnp.float32),
             pltpu.VMEM((souths, I, M), jnp.float32),
             pltpu.SemaphoreType.REGULAR((max(1, (souths - 1).bit_length()),)),
-            dma((4,)), dma((2,)), dma((2,)), dma((2,)), dma((2,)), dma((2,)), dma, dma((2,)), pltpu.SemaphoreType.REGULAR,
+            dma((4,)), dma, dma((2,)), dma((2,)), dma((2,)), dma((2,)), dma, pltpu.SemaphoreType.REGULAR,
         ],
         compiler_params=pltpu.CompilerParams(collective_id=0, has_side_effects=True,
                                              vmem_limit_bytes=106 * 2 ** 19),
@@ -528,7 +527,7 @@
         out_shape=(out, out),
         in_specs=[pl.BlockSpec(memory_space=pltpu.VMEM)] * 2,
         out_specs=(pl.BlockSpec(memory_space=pl.ANY),) * 2,
-        scratch_shapes=[pltpu.VMEM((J, I, M), jnp.float32), pltpu.SemaphoreType.DMA((3,))],
+        scratch_shapes=[pltpu.VMEM((J, I, M), jnp.float32), pltpu.SemaphoreType.DMA((2,))],
         compiler_params=pltpu.CompilerParams(vmem_limit_bytes=2 ** 21),
     )(*results)
 

time: 13.8 us -> 13.7 us (level)
  no operation moved by 1% of the time
where the time goes in v6:
time: 13.7 us; the launch traced here: 13.6 us
  Pallas kernels  12.9 us (94%)
  between operations  0.64 us (5%)
    pallas_call x1, Pallas kernels, per_device(): pl.pallas_call(functools.partial(kernel, souths, easts), out_shape=(jax.S...  12 us
    pallas_call x1, Pallas kernels, per_device(): pl.pallas_call(functools.partial(write_out, 1.0 / (J * souths)), out_shap...  0.98 us

profile of v6, /device:TPU:24, one launch (start us, length us, event | category | flops | bytes accessed | tf_op | source)
XLA Modules:
  0.0 13.6 jit_solution(18096274185623836071)
XLA Ops:
  0.6 12.0 %shard_map.50 = (f32[32,128]{1,0:T(8,128)S(1)}, f32[32,32,128]{2,1,0:T(8,128)S(1)}) custom-call(f32[32,32,128]{2,1,0:T(8,128)} %tracer.1, f32[32,32,128]{2,1,0:T(8,128)} %flow_j.1, f32[32,32,128]{2,1,0:T(8,128)} %flow_i.1), custom_call_target="tpu_custom_call" | custom-call | tf_op jit(solution)/shard_map/pallas_call | solution.py:500
  12.6 1.0 %shard_map.51 = (f32[32,32,128]{2,1,0:T(8,128)}, f32[32,32,128]{2,1,0:T(8,128)}) custom-call(f32[32,128]{1,0:T(8,128)S(1)} %get-tuple-element.4.before, f32[32,32,128]{2,1,0:T(8,128)S(1)} %get-tuple-element.5.end), custom_call_target="tpu_custom_call" | custom-call | tf_op jit(solution)/shard_map/pallas_call | solution.py:525
